TPU v7x, 256 devices: a whole 4x4x8 slice. The times are simulated.
256 devices in a mesh: lon: 32 (over x_hi, z, core), lat: 8 (over y, x_lo).
Axes of the slice: x: 4 (x_hi: 2, x_lo: 2; x = x_hi * 2 + x_lo), y: 4, z: 8, core: 2. Of those that a mesh axis runs over, the one named last changes fastest.
Arguments:
- tokens: bfloat16 [2, 96, 147456], P(None, 'lat', 'lon'), may hold values from -6 to 6
- cotangent: bfloat16 [2, 48, 147456], P(None, 'lat', 'lon'), may hold values from -6 to 6
- kinds_one: int32 [1, 16], P(None, 'lat'), may hold values from 0 to 7
- kinds_two: int32 [1, 8], P(None, 'lat'), may hold values from 0 to 7
- table_one: float32 [8, 6, 3312], replicated, may hold values from -2 to 260
- table_two: float32 [8, 12, 3312], replicated, may hold values from -2 to 260
- gain_one: float32 [192], replicated, may hold values from 0.1 to 1.9
- gain_merge: float32 [768], replicated, may hold values from 0.1 to 1.9
- gain_two: float32 [384], replicated, may hold values from 0.1 to 1.9
- qkv_one: bfloat16 [192, 576], replicated, may hold values from -0.4375 to 0.4375
- proj_one: bfloat16 [192, 192], replicated, may hold values from -0.4375 to 0.4375
- merge_weight: bfloat16 [768, 384], replicated, may hold values from -0.21875 to 0.21875
- qkv_two: bfloat16 [384, 1152], replicated, may hold values from -0.3125 to 0.3125
- proj_two: bfloat16 [384, 384], replicated, may hold values from -0.3125 to 0.3125
Outputs:
- result: bfloat16 [2, 48, 147456], P(None, 'lat', 'lon')
- d_tokens: bfloat16 [2, 96, 147456], P(None, 'lat', 'lon')
- grad_qkv_one: bfloat16 [192, 576], replicated
- grad_proj_one: bfloat16 [192, 192], replicated
- grad_merge: bfloat16 [768, 384], replicated
- grad_qkv_two: bfloat16 [384, 1152], replicated
- grad_proj_two: bfloat16 [384, 384], replicated
All inputs are finite; a program needn't handle non-finite values.
Results may differ from a plain program's by a relative error of at most 0.025.
Values may be sent and summed in bfloat16 or wider, within the bound.
A program may use at most 128 MiB of HBM per device.

v0:
```python
import jax
import jax.numpy as jnp
import numpy as np
from jax import lax
from jax.sharding import PartitionSpec as P

C1 = 192
HEADS1 = 6
HEADS2 = 12
WIN_Z = 2
WIN_LAT = 6
WIN_LON = 12
LEVELS = 2
norm_epsilon = 1e-05
grad_epsilon = 1e-06
masked_score = -1e30


def as_sent(value):
    return jax.tree.map(lambda a: a.astype(jnp.bfloat16) if a.dtype == jnp.float32 else a, value)


def shifted_2(block, axis, distance):
    devices = range(lax.axis_size(axis))
    route = [((i - distance) % len(devices), i) for i in devices]
    return lax.ppermute(block, axis, route)


def relative_table():
    window_size = WIN_Z * WIN_LAT * WIN_LON
    positions = np.arange(window_size)
    level_at = positions // (WIN_LAT * WIN_LON)
    row_at = positions // WIN_LON % WIN_LAT
    col_at = positions % WIN_LON
    joined = (level_at[:, None] * WIN_Z + level_at[None, :]) * (WIN_LAT * WIN_LAT)
    joined = joined + row_at[:, None] * WIN_LAT + row_at[None, :]
    joined = joined * (2 * WIN_LON - 1) + col_at[:, None] - col_at[None, :] + WIN_LON - 1
    return joined.astype(np.int32)


def layer_norm(values, scaling):
    centre = jnp.mean(values, axis=-1, keepdims=True)
    spread = values - centre
    second = jnp.mean(spread * spread, axis=-1, keepdims=True)
    return spread * lax.rsqrt(second + norm_epsilon) * scaling


def to_windows(lattice):
    level_count, row_count, col_count = lattice.shape[:3]
    trailing = lattice.shape[3:]
    trailing_axes = tuple(range(6, 6 + len(trailing)))
    pieces = lattice.reshape(
        (level_count // WIN_Z, WIN_Z, row_count // WIN_LAT, WIN_LAT, col_count // WIN_LON, WIN_LON)
        + trailing
    )
    pieces = pieces.transpose((0, 2, 4, 1, 3, 5) + trailing_axes)
    return pieces.reshape(
        (
            level_count // WIN_Z,
            row_count // WIN_LAT,
            col_count // WIN_LON,
            WIN_Z * WIN_LAT * WIN_LON,
        )
        + trailing
    )


def from_windows(blocks, level_count, row_count, col_count):
    trailing = blocks.shape[4:]
    trailing_axes = tuple(range(6, 6 + len(trailing)))
    pieces = blocks.reshape(
        (level_count // WIN_Z, row_count // WIN_LAT, col_count // WIN_LON, WIN_Z, WIN_LAT, WIN_LON)
        + trailing
    )
    pieces = pieces.transpose((0, 3, 1, 4, 2, 5) + trailing_axes)
    return pieces.reshape((level_count, row_count, col_count) + trailing)


def region_codes(level_count, row_start, row_count, rows_all):
    level_index = jnp.arange(level_count, dtype=jnp.int32)
    level_part = (level_index >= level_count - WIN_Z).astype(jnp.int32) + (
        level_index >= level_count - WIN_Z // 2
    ).astype(jnp.int32)
    row_index = row_start + jnp.arange(row_count, dtype=jnp.int32)
    row_part = (row_index >= rows_all - WIN_LAT).astype(jnp.int32) + (
        row_index >= rows_all - WIN_LAT // 2
    ).astype(jnp.int32)
    return level_part[:, None] * 3 + row_part[None, :]


def attend(
    shifted,
    kind_ids,
    bias_table,
    scaling,
    w_qkv,
    w_proj,
    head_count,
    row_start,
    rows_all,
    probe_qkv,
    probe_proj,
):
    level_count, row_count, col_count, channel_count = shifted.shape
    head_size = channel_count // head_count
    base_values = shifted.astype(jnp.float32)
    normed = layer_norm(base_values, scaling).astype(jnp.bfloat16)
    flat_rows = normed.reshape(-1, channel_count)
    packed = (jnp.dot(flat_rows, w_qkv, preferred_element_type=jnp.float32) + probe_qkv).astype(
        jnp.bfloat16
    )
    packed = to_windows(packed.reshape(level_count, row_count, col_count, 3, head_count, head_size))
    query_rows = packed[..., 0, :, :]
    key_rows = packed[..., 1, :, :]
    value_rows = packed[..., 2, :, :]
    scores = jnp.einsum(
        "abdqhe,abdkhe->abdhqk", query_rows, key_rows, preferred_element_type=jnp.float32
    ) * head_size ** (-0.5)
    chosen = bias_table[kind_ids]
    full_bias = jnp.take(chosen, relative_table(), axis=3)
    scores = scores + full_bias[:, :, None]
    region_ids = region_codes(level_count, row_start, row_count, rows_all)
    tag_values = jnp.broadcast_to(
        region_ids[:, :, None], (level_count, row_count, col_count)
    ).astype(jnp.float32)
    window_tags = to_windows(tag_values)
    allowed = window_tags[..., :, None] == window_tags[..., None, :]
    scores = jnp.where(allowed[:, :, :, None], scores, masked_score)
    row_top = jnp.max(scores, axis=-1, keepdims=True)
    weights = jnp.exp(scores - row_top)
    attn_weights = (weights / jnp.sum(weights, axis=-1, keepdims=True)).astype(jnp.bfloat16)
    attended = jnp.einsum(
        "abdhqk,abdkhe->abdqhe", attn_weights, value_rows, preferred_element_type=jnp.float32
    ).astype(jnp.bfloat16)
    merged_rows = from_windows(attended, level_count, row_count, col_count).reshape(
        -1, channel_count
    )
    result = (
        base_values.reshape(-1, channel_count)
        + jnp.dot(merged_rows, w_proj, preferred_element_type=jnp.float32)
        + probe_proj
    )
    return (result.astype(jnp.bfloat16).reshape(shifted.shape), (flat_rows, merged_rows))


def merge_tokens(level_one, scaling, w_merge, probe_merge):
    level_count, row_count, col_count, channel_count = level_one.shape
    grouped = level_one.reshape(level_count, row_count // 2, 2, col_count // 2, 2, channel_count)
    grouped = grouped.transpose(0, 1, 3, 2, 4, 5).reshape(
        level_count, row_count // 2, col_count // 2, 4 * channel_count
    )
    normed = layer_norm(grouped.astype(jnp.float32), scaling).astype(jnp.bfloat16)
    flat_rows = normed.reshape(-1, 4 * channel_count)
    merged = (jnp.dot(flat_rows, w_merge, preferred_element_type=jnp.float32) + probe_merge).astype(
        jnp.bfloat16
    )
    return (
        merged.reshape(level_count, row_count // 2, col_count // 2, w_merge.shape[1]),
        flat_rows,
    )


def weight_grad(inputs, cot_rows):
    return lax.dot_general(
        inputs,
        cot_rows.astype(jnp.bfloat16),
        (((0,), (0,)), ((), ())),
        preferred_element_type=jnp.float32,
    )


def normalized(gradient):
    scale_back = lax.rsqrt(jnp.mean(gradient * gradient) + grad_epsilon)
    return (gradient * scale_back).astype(jnp.bfloat16)


def lat_move(band_piece, offset):
    return jax.tree.map(
        lambda part, own: part.astype(own.dtype),
        shifted_2(as_sent(band_piece), "lat", offset),
        band_piece,
    )


def lon_move(band_piece, offset):
    return shifted_2(as_sent(band_piece), "lon", offset).astype(band_piece.dtype)


def roll_ahead(lattice, level_step):
    half_lat = WIN_LAT // 2
    half_lon = WIN_LON // 2
    if level_step != 0:
        lattice = jnp.roll(lattice, -level_step, 0)
    lattice = jnp.concatenate([lattice[:, half_lat:], lat_move(lattice[:, :half_lat], -1)], 1)
    return jnp.concatenate([lattice[:, :, half_lon:], lon_move(lattice[:, :, :half_lon], -1)], 2)


def roll_behind(lattice, level_step):
    half_lat = WIN_LAT // 2
    half_lon = WIN_LON // 2
    lattice = jnp.concatenate([lat_move(lattice[:, -half_lat:], 1), lattice[:, :-half_lat]], 1)
    lattice = jnp.concatenate(
        [lon_move(lattice[:, :, -half_lon:], 1), lattice[:, :, :-half_lon]], 2
    )
    if level_step != 0:
        lattice = jnp.roll(lattice, level_step, 0)
    return lattice


def local_pass(shifted, kind_ids, bias_table, scaling, w_qkv, w_proj, head_count):
    level_count, row_count, col_count, channel_count = shifted.shape
    token_count = level_count * row_count * col_count
    row_start = lax.axis_index("lat") * row_count
    rows_all = lax.axis_size("lat") * row_count

    def local_forward(lattice, probe_qkv, probe_proj):
        return attend(
            lattice,
            kind_ids,
            bias_table,
            scaling,
            w_qkv,
            w_proj,
            head_count,
            row_start,
            rows_all,
            probe_qkv,
            probe_proj,
        )

    return jax.vjp(
        local_forward,
        shifted,
        jnp.zeros((token_count, 3 * channel_count), jnp.float32),
        jnp.zeros((token_count, channel_count), jnp.float32),
        has_aux=True,
    )


def merge_pass(level_one, scaling, w_merge):
    token_count = level_one.shape[0] * (level_one.shape[1] // 2) * (level_one.shape[2] // 2)

    def merge_forward(lattice, probe_merge):
        return merge_tokens(lattice, scaling, w_merge, probe_merge)

    return jax.vjp(
        merge_forward,
        level_one,
        jnp.zeros((token_count, w_merge.shape[1]), jnp.float32),
        has_aux=True,
    )


def shards(
    tokens,
    cotangent,
    kinds_one,
    kinds_two,
    table_one,
    table_two,
    gain_one,
    gain_merge,
    gain_two,
    qkv_one,
    proj_one,
    merge_weight,
    qkv_two,
    proj_two,
):
    row_count = tokens.shape[1]
    col_count = tokens.shape[2] // C1
    level_step = WIN_Z // 2
    lattice = tokens.reshape(LEVELS, row_count, col_count, C1)
    shifted_one = roll_ahead(lattice, level_step)
    block_one, pull_one, saved_one = local_pass(
        shifted_one, kinds_one, table_one, gain_one, qkv_one, proj_one, HEADS1
    )
    moved_one = roll_ahead(block_one, 0)
    shifted_two, pull_merge, merged_norm = merge_pass(moved_one, gain_merge, merge_weight)
    block_two, pull_two, saved_two = local_pass(
        shifted_two, kinds_two, table_two, gain_two, qkv_two, proj_two, HEADS2
    )
    level_two = roll_behind(block_two, level_step)
    d_block_two = roll_ahead(cotangent.reshape(level_two.shape), level_step)
    d_shift_two, d_packed_two, d_out_two = pull_two(d_block_two)
    raw_qkv_two = weight_grad(saved_two[0], d_packed_two)
    raw_proj_two = weight_grad(saved_two[1], d_out_two)
    d_moved_one, d_probe_merge = pull_merge(d_shift_two)
    raw_merge = weight_grad(merged_norm, d_probe_merge)
    d_block_one = roll_behind(d_moved_one, 0)
    d_shift_one, d_packed_one, d_out_one = pull_one(d_block_one)
    raw_qkv_one = weight_grad(saved_one[0], d_packed_one)
    raw_proj_one = weight_grad(saved_one[1], d_out_one)
    d_tokens = roll_behind(d_shift_one, level_step)
    raw_qkv_one, raw_proj_one, raw_merge, raw_qkv_two, raw_proj_two = lax.psum(
        (raw_qkv_one, raw_proj_one, raw_merge, raw_qkv_two, raw_proj_two), ("lon", "lat")
    )
    return (
        level_two.reshape(LEVELS, level_two.shape[1], -1),
        d_tokens.reshape(LEVELS, row_count, -1),
        normalized(raw_qkv_one),
        normalized(raw_proj_one),
        normalized(raw_merge),
        normalized(raw_qkv_two),
        normalized(raw_proj_two),
    )


def solution(mesh):
    in_specs = (
        P(None, "lat", "lon"),
        P(None, "lat", "lon"),
        P(None, "lat"),
        P(None, "lat"),
        P(),
        P(),
        P(),
        P(),
        P(),
        P(),
        P(),
        P(),
        P(),
        P(),
    )
    out_specs = (P(None, "lat", "lon"), P(None, "lat", "lon"), P(), P(), P(), P(), P())
    return jax.shard_map(shards, mesh=mesh, in_specs=in_specs, out_specs=out_specs, check_vma=False)
```

profile of v0, /device:TPU:8, one launch (start us, length us, event | category | flops | bytes accessed | tf_op | source)
XLA Modules:
  0.0 644.9 jit_solution(7995490828892708729)
XLA Ops:
  21.4 4.5 copy.138
  25.9 55.6 %gather_fusion.1 = f32[20736,2,6]{2,1,0:T(2,128)} fusion(f32[2,6,3312]{1,0,2:T(2,128)S(1)} %copy.138, s32[21504]{0:T(1024)S(1)} %pad_clamp_fusion), kind=kCustom, calls=%fused_computation.1 | custom fusion | bytes 2073600 | tf_op jit(solution)/shard_map/jvp(jit(_take))/gather | solution.py:120
  81.5 31.0 %copy.139 = f32[144,144,2,6]{0,1,3,2:T(8,128)} copy(f32[144,144,2,6]{3,2,1,0:T(2,128)} %bitcast.176) | data formatting | bytes 1990656 | tf_op jit(solution)/shard_map/jvp(jit(_take))/gather | solution.py:120
  113.1 38.8 %gather_fusion.2 = f32[20736,12]{1,0:T(8,128)} fusion(f32[12,3312]{0,1:T(8,128)S(1)} %bitcast.170, s32[21504]{0:T(1024)S(1)} %pad_clamp_fusion), kind=kCustom, calls=%fused_computation.2 | custom fusion | bytes 2073600 | tf_op jit(solution)/shard_map/jvp(jit(_take))/gather | solution.py:120
  151.9 12.2 %copy.152 = f32[144,144,12]{0,1,2:T(8,128)} copy(f32[144,144,12]{2,1,0:T(8,128)} %bitcast.177) | data formatting | bytes 1990656 | tf_op jit(solution)/shard_map/jvp(jit(_take))/gather | solution.py:120
  164.8 5.6 collective-permute-start.1
  177.0 3.9 reshape.727
  180.9 2.7 copy.134
  183.7 2.6 fusion.95
  190.2 2.9 fusion.5
  194.1 3.5 convert_reduce_fusion
  197.6 3.0 copy.192
  200.6 2.7 fusion.23
  203.4 3.1 copy.141
  206.4 2.5 copy.142
  208.9 2.6 reshape.733
  216.9 3.4 collective-permute-start.2
  231.2 5.0 collective-permute-start.3
  285.0 3.0 fusion.86
  301.6 2.6 convolution_bitcast_fusion
  307.8 6.7 %collective-permute-done.9 = bf16[2,12,6,192]{3,2,1,0:T(8,128)(2,1)S(1)} collective-permute-done((bf16[2,12,6,192]{3,2,1,0:T(8,128)(2,1)S(1)}, bf16[2,12,6,192]{3,2,1,0:T(8,128)(2,1)S(1)}, u32[]{:S(2)}, u32[]{:S(2)}) %collective-permute-start.9) | collective-permute-done | bytes 55328 | tf_op jit(solution)/shard_map/ppermute | solution.py:26
  318.1 2.4 reshape.747
  320.5 3.1 copy.165
  323.6 3.0 copy.166
  326.6 3.4 fusion.3
  335.4 4.9 copy.171
  340.3 2.5 copy.172
  342.8 2.9 reshape.751
  353.5 4.9 collective-permute-done.4
  358.7 7.3 %collective-permute-done.5 = bf16[2,6,6,384]{3,2,1,0:T(8,128)(2,1)S(1)} collective-permute-done((bf16[2,6,6,384]{3,2,1,0:T(8,128)(2,1)S(1)}, bf16[2,6,6,384]{3,2,1,0:T(8,128)(2,1)S(1)}, u32[]{:S(2)}, u32[]{:S(2)}) %collective-permute-start.5) | collective-permute-done | bytes 55328 | tf_op jit(solution)/shard_map/ppermute | solution.py:26
  367.2 6.9 %collective-permute-done.11 = bf16[2,12,6,192]{3,2,1,0:T(8,128)(2,1)S(1)} collective-permute-done((bf16[2,12,6,192]{3,2,1,0:T(8,128)(2,1)S(1)}, bf16[2,12,6,192]{3,2,1,0:T(8,128)(2,1)S(1)}, u32[]{:S(2)}, u32[]{:S(2)}) %collective-permute-start.11) | collective-permute-done | bytes 55328 | tf_op jit(solution)/shard_map/ppermute | solution.py:26
  375.6 245.0 %all-reduce.9.cloned.1.call-done = (f32[192,576]{1,0:T(8,128)}, f32[192,192]{1,0:T(8,128)}, f32[768,384]{1,0:T(8,128)}, f32[384,1152]{1,0:T(8,128)}, f32[384,384]{1,0:T(8,128)}) async-done(((f32[192,576]{1,0:T(8,128)}, f32[192,192]{1,0:T(8,128)}, f32[768,384]{1,0:T(8,128)}, f32[384,1152]{1,0:T(8,128)}, f32[384,384]{1,0:T(8,128)}), (f32[192,576]{1,0:T(8,128)}, f32[192,192]{1,0:T(8,128)}, ...) | async-done | bytes 4128784 | tf_op jit(solution)/shard_map/psum | solution.py:295
  (347 shorter events, 140.9 us)
Async XLA Ops:
  7.2 11.0 %copy-start = (f32[8,12,3312]{2,0,1:T(8,128)S(1)}, f32[8,12,3312]{2,0,1:T(8,128)}, u32[]{:S(2)}) copy-start(f32[8,12,3312]{2,0,1:T(8,128)} %param.21) | copy-start | bytes 3815428
  7.2 8.2 %copy-start.64 = (s32[20736]{0:T(1024)S(1)}, s32[20736]{0:T(1024)}, u32[]{:S(2)}) copy-start(s32[20736]{0:T(1024)} %constant.166) | copy-start | bytes 248836
  7.2 4.6 copy-start.55
  7.2 8.2 %copy-start.81 = (s32[1,2]{1,0:T(1,128)S(1)}, s32[1,2]{1,0:T(1,128)}, u32[]{:S(2)}) copy-start(s32[1,2]{1,0:T(1,128)} %param.18) | copy-start | bytes 28
  7.2 613.3 %all-reduce.9.cloned.1.call-start = ((), (), s32[]{:S(2)}) async-start(), calls=%async_computation | async-start | bytes 8454144 | tf_op jit(solution)/shard_map/psum | solution.py:295
  9.6 10.1 %copy-start.18 = (f32[8,6,3312]{2,0,1:T(8,128)S(1)}, f32[8,6,3312]{2,0,1:T(8,128)}, u32[]{:S(2)}) copy-start(f32[8,6,3312]{2,0,1:T(8,128)} %param.20) | copy-start | bytes 1907716
  10.4 154.3 %collective-permute-start = (bf16[2,3,24,192]{3,2,1,0:T(8,128)(2,1)}, bf16[2,3,24,192]{3,2,1,0:T(8,128)(2,1)S(1)}, u32[]{:S(2)}, u32[]{:S(2)}) collective-permute-start(bf16[2,3,24,192]{3,2,1,0:T(8,128)(2,1)} %slice.192), channel_id=1, source_target_pairs={{1,0},{2,1},{3,2},{4,3},{5,4},{6,5},{7,6},{0,7},{9,8},{10,9},{11,1... | collective-permute-start | bytes 165896 | tf_op jit(solution)/shard_map/ppermute | solution.py:26
  13.2 157.2 %collective-permute-start.6 = (bf16[2,3,12,384]{3,2,1,0:T(8,128)(2,1)}, bf16[2,3,12,384]{3,2,1,0:T(8,128)(2,1)}, u32[]{:S(2)}, u32[]{:S(2)}) collective-permute-start(bf16[2,3,12,384]{3,2,1,0:T(8,128)(2,1)} %get-tuple-element.59), channel_id=1, source_target_pairs={{1,0},{2,1},{3,2},{4,3},{5,4},{6,5},{7,6},{0,7},{9,8},{10,9},{11,1... | collective-permute-start | bytes 165896 | tf_op jit(solution)/shard_map/ppermute | solution.py:26
  81.5 31.0 %copy-start.49 = (f32[1,12,3312]{2,0,1:T(1,128)S(1)}, f32[1,12,3312]{2,0,1:T(1,128)}, u32[]{:S(2)}) copy-start(f32[1,12,3312]{2,0,1:T(1,128)} %constant_dynamic-slice_fusion) | copy-start | bytes 476932
  151.9 12.2 %copy-start.69 = (f32[768]{0:T(1024)S(1)}, f32[768]{0:T(1024)}, u32[]{:S(2)}) copy-start(f32[768]{0:T(1024)} %param.23) | copy-start | bytes 9220
  151.9 12.8 %copy-start.29 = (bf16[2,9,24,192]{3,2,1,0:T(8,128)(2,1)S(1)}, bf16[2,9,24,192]{3,2,1,0:T(8,128)(2,1)}, u32[]{:S(2)}) copy-start(bf16[2,9,24,192]{3,2,1,0:T(8,128)(2,1)} %slice.191) | copy-start | bytes 497668
  151.9 18.4 %copy-start.59 = (bf16[2,3,12,384]{3,2,1,0:T(8,128)(2,1)S(1)}, bf16[2,3,12,384]{3,2,1,0:T(8,128)(2,1)}, u32[]{:S(2)}) copy-start(bf16[2,3,12,384]{3,2,1,0:T(8,128)(2,1)} %get-tuple-element.58) | copy-start | bytes 165892
  164.8 8.6 %collective-permute-start.1 = (bf16[2,12,6,192]{3,2,1,0:T(8,128)(2,1)S(1)}, bf16[2,12,6,192]{3,2,1,0:T(8,128)(2,1)S(1)}, u32[]{:S(2)}, u32[]{:S(2)}) collective-permute-start(bf16[2,12,6,192]{3,2,1,0:T(8,128)(2,1)S(1)} %pad_maximum_fusion.9), channel_id=1, source_target_pairs={{8,0},{16,8},{24,16},{32,24},{40,32},{48,40},{56,48},{64,56},{72,6... | collective-permute-start | bytes 165896 | tf_op jit(solution)/shard_map/ppermute | solution.py:26
  171.9 3.7 copy-start.46
  171.9 3.7 copy-start.75
  171.9 48.5 %collective-permute-start.7 = (bf16[2,6,6,384]{3,2,1,0:T(8,128)(2,1)}, bf16[2,6,6,384]{3,2,1,0:T(8,128)(2,1)}, u32[]{:S(2)}, u32[]{:S(2)}) collective-permute-start(bf16[2,6,6,384]{3,2,1,0:T(8,128)(2,1)} %get-tuple-element.57), channel_id=1, source_target_pairs={{8,0},{16,8},{24,16},{32,24},{40,32},{48,40},{56,48},{64,56},{72,6... | collective-permute-start | bytes 165896 | tf_op jit(solution)/shard_map/ppermute | solution.py:26
  194.1 3.5 copy-start.52
  216.9 13.3 %collective-permute-start.2 = (bf16[2,3,24,192]{3,2,1,0:T(8,128)(2,1)}, bf16[2,3,24,192]{3,2,1,0:T(8,128)(2,1)}, u32[]{:S(2)}, u32[]{:S(2)}) collective-permute-start(bf16[2,3,24,192]{3,2,1,0:T(8,128)(2,1)} %slice.199), channel_id=1, source_target_pairs={{1,0},{2,1},{3,2},{4,3},{5,4},{6,5},{7,6},{0,7},{9,8},{10,9},{11,1... | collective-permute-start | bytes 165896 | tf_op jit(solution)/shard_map/ppermute | solution.py:26
  231.2 7.2 %collective-permute-start.3 = (bf16[2,12,6,192]{3,2,1,0:T(8,128)(2,1)S(1)}, bf16[2,12,6,192]{3,2,1,0:T(8,128)(2,1)S(1)}, u32[]{:S(2)}, u32[]{:S(2)}) collective-permute-start(bf16[2,12,6,192]{3,2,1,0:T(8,128)(2,1)S(1)} %pad_maximum_fusion.8), channel_id=1, source_target_pairs={{8,0},{16,8},{24,16},{32,24},{40,32},{48,40},{56,48},{64,56},{72,6... | collective-permute-start | bytes 165896 | tf_op jit(solution)/shard_map/ppermute | solution.py:26
  298.5 7.1 %collective-permute-start.8 = (bf16[2,3,24,192]{3,2,1,0:T(8,128)(2,1)}, bf16[2,3,24,192]{3,2,1,0:T(8,128)(2,1)}, u32[]{:S(2)}, u32[]{:S(2)}) collective-permute-start(bf16[2,3,24,192]{3,2,1,0:T(8,128)(2,1)} %copy.195), channel_id=1, source_target_pairs={{7,0},{0,1},{1,2},{2,3},{3,4},{4,5},{5,6},{6,7},{15,8},{8,9},{9,10... | collective-permute-start | bytes 165896 | tf_op jit(solution)/shard_map/ppermute | solution.py:26
  301.6 3.8 copy-start.44
  304.2 11.1 %copy-start.58 = (bf16[192,192]{1,0:T(8,128)(2,1)S(1)}, bf16[192,192]{1,0:T(8,128)(2,1)}, u32[]{:S(2)}) copy-start(bf16[192,192]{1,0:T(8,128)(2,1)} %param.26) | copy-start | bytes 221188
  305.4 9.1 %copy-start.32 = (bf16[12,32,144]{2,1,0:T(8,128)(2,1)}, bf16[12,32,144]{2,1,0:T(8,128)(2,1)S(1)}, u32[]{:S(2)}) copy-start(bf16[12,32,144]{2,1,0:T(8,128)(2,1)S(1)} %convolution_convert_fusion.12) | copy-start | bytes 331780
  306.5 7.9 %copy-start.30 = (bf16[2,12,24,192]{3,2,1,0:T(8,128)(2,1)}, bf16[2,12,24,192]{3,2,1,0:T(8,128)(2,1)S(1)}, u32[]{:S(2)}) copy-start(bf16[2,12,24,192]{3,2,1,0:T(8,128)(2,1)S(1)} %copy_dynamic-update-slice_fusion) | copy-start | bytes 663556
  306.6 7.8 %collective-permute-start.9 = (bf16[2,12,6,192]{3,2,1,0:T(8,128)(2,1)S(1)}, bf16[2,12,6,192]{3,2,1,0:T(8,128)(2,1)S(1)}, u32[]{:S(2)}, u32[]{:S(2)}) collective-permute-start(bf16[2,12,6,192]{3,2,1,0:T(8,128)(2,1)S(1)} %slice.217), channel_id=1, source_target_pairs={{248,0},{0,8},{8,16},{16,24},{24,32},{32,40},{40,48},{48,56},{56,6... | collective-permute-start | bytes 165896 | tf_op jit(solution)/shard_map/ppermute | solution.py:26
  352.9 5.6 collective-permute-start.4
  358.5 7.5 %collective-permute-start.5 = (bf16[2,6,6,384]{3,2,1,0:T(8,128)(2,1)S(1)}, bf16[2,6,6,384]{3,2,1,0:T(8,128)(2,1)S(1)}, u32[]{:S(2)}, u32[]{:S(2)}) collective-permute-start(bf16[2,6,6,384]{3,2,1,0:T(8,128)(2,1)S(1)} %fusion.69), channel_id=1, source_target_pairs={{248,0},{0,8},{8,16},{16,24},{24,32},{32,40},{40,48},{48,56},{56,6... | collective-permute-start | bytes 165896 | tf_op jit(solution)/shard_map/ppermute | solution.py:26
  358.6 7.5 %collective-permute-start.10 = (bf16[2,3,24,192]{3,2,1,0:T(8,128)(2,1)S(1)}, bf16[2,3,24,192]{3,2,1,0:T(8,128)(2,1)S(1)}, u32[]{:S(2)}, u32[]{:S(2)}) collective-permute-start(bf16[2,3,24,192]{3,2,1,0:T(8,128)(2,1)S(1)} %slice.219), channel_id=1, source_target_pairs={{7,0},{0,1},{1,2},{2,3},{3,4},{4,5},{5,6},{6,7},{15,8},{8,9},{9,10... | collective-permute-start | bytes 165896 | tf_op jit(solution)/shard_map/ppermute | solution.py:26
  366.2 7.9 %collective-permute-start.11 = (bf16[2,12,6,192]{3,2,1,0:T(8,128)(2,1)S(1)}, bf16[2,12,6,192]{3,2,1,0:T(8,128)(2,1)S(1)}, u32[]{:S(2)}, u32[]{:S(2)}) collective-permute-start(bf16[2,12,6,192]{3,2,1,0:T(8,128)(2,1)S(1)} %pad_maximum_fusion.7), channel_id=1, source_target_pairs={{248,0},{0,8},{8,16},{16,24},{24,32},{32,40},{40,48},{48,56},{56,6... | collective-permute-start | bytes 165896 | tf_op jit(solution)/shard_map/ppermute | solution.py:26
  620.5 8.3 %copy-start.17 = (f32[768,384]{1,0:T(8,128)S(1)}, f32[768,384]{1,0:T(8,128)}, u32[]{:S(2)}) copy-start(f32[768,384]{1,0:T(8,128)} %get-tuple-element.31) | copy-start | bytes 3538948
  624.8 6.5 %copy-start.14 = (f32[384,1152]{1,0:T(8,128)S(1)}, f32[384,1152]{1,0:T(8,128)}, u32[]{:S(2)}) copy-start(f32[384,1152]{1,0:T(8,128)} %get-tuple-element.32) | copy-start | bytes 5308420
  633.0 4.8 copy-start.1
  (63 other events, 103.1 us)
Sparse Core Ops, SparseCore 0:
  351.6 268.9 all-reduce.8
where the time goes:
time: 656 us; the launch traced here: 645 us
  waiting for transfers between devices  272 us (41%)
  local copies, waits for them, and re-layouts  246 us (38%)
  other arithmetic  46.4 us (7%)
  matrix products  40.4 us (6%)
  starting transfers between devices  20.1 us (3%)
  between operations  19.7 us (3%)
    psum x1, waiting for transfers between devices, shards(): lax.psum((raw_qkv_one, raw_proj_one, raw_merge, raw_qkv_two, raw_proj_two...  245 us
    gather x4, local copies, waits for them, and re-layouts, attend(): full_bias = jnp.take(chosen, relative_table(), axis=3)  138 us
    ppermute x12, waiting for transfers between devices, shifted_2(): return lax.ppermute(block, axis, route)  27 us
    ppermute x12, starting transfers between devices, shifted_2(): return lax.ppermute(block, axis, route)  20.1 us
    unnamed x171, local copies, waits for them, and re-layouts  18.2 us
  transfers between devices with their start and end apart: 13, of which 6 were waited for; matrix products, arithmetic and copies ran while one was open for 33% of the time, Pallas kernels for 0%

commit v1 on v0

--- a/solution.py
+++ b/solution.py
@@ -293,7 +293,7 @@
     raw_proj_one = weight_grad(saved_one[1], d_out_one)
     d_tokens = roll_behind(d_shift_one, level_step)
     raw_qkv_one, raw_proj_one, raw_merge, raw_qkv_two, raw_proj_two = lax.psum(
-        (raw_qkv_one, raw_proj_one, raw_merge, raw_qkv_two, raw_proj_two), ("lon", "lat")
+        lax.psum((raw_qkv_one, raw_proj_one, raw_merge, raw_qkv_two, raw_proj_two), "lon"), "lat"
     )
     return (
         level_two.reshape(LEVELS, level_two.shape[1], -1),

time: 656 us -> 851 us (1.30)
  waiting for transfers between devices: 272 us -> 465 us
    psum x0 -> x1, waiting for transfers between devices: none -> 164 us  [shards(): lax.psum(lax.psum((raw_qkv_one, raw_proj_one, raw_merge, raw_qkv_two, raw...]
    psum x1, waiting for transfers between devices: 245 us -> 275 us  [shards(): lax.psum((raw_qkv_one, raw_proj_one, raw_merge, raw_qkv_two, raw_proj_two...]
  transfers between devices with their start and end apart: 13 -> 14, of which waited for: 6 -> 7; matrix products, arithmetic and copies ran while one was open for 33% -> 26% of each run, Pallas kernels for 0% -> 0%
where the time goes in v1:
time: 851 us; the launch traced here: 839 us
  waiting for transfers between devices  465 us (55%)
  local copies, waits for them, and re-layouts  246 us (29%)
  other arithmetic  46.4 us (5%)
  matrix products  40.4 us (5%)
  starting transfers between devices  21.7 us (3%)
  between operations  19.7 us (2%)
    psum x1, waiting for transfers between devices, shards(): lax.psum((raw_qkv_one, raw_proj_one, raw_merge, raw_qkv_two, raw_proj_two...  275 us
    psum x1, waiting for transfers between devices, shards(): lax.psum(lax.psum((raw_qkv_one, raw_proj_one, raw_merge, raw_qkv_two, raw...  164 us
    gather x4, local copies, waits for them, and re-layouts, attend(): full_bias = jnp.take(chosen, relative_table(), axis=3)  138 us
    ppermute x12, waiting for transfers between devices, shifted_2(): return lax.ppermute(block, axis, route)  25.5 us
    ppermute x12, starting transfers between devices, shifted_2(): return lax.ppermute(block, axis, route)  21.6 us
    unnamed x171, local copies, waits for them, and re-layouts  18.2 us
  transfers between devices with their start and end apart: 14, of which 7 were waited for; matrix products, arithmetic and copies ran while one was open for 26% of the time, Pallas kernels for 0%

profile of v1, /device:TPU:8, one launch (start us, length us, event | category | flops | bytes accessed | tf_op | source)
XLA Modules:
  0.0 839.1 jit_solution(15603349317365039086)
XLA Ops:
  21.4 4.5 copy.138
  25.9 55.7 %gather_fusion.1 = f32[20736,2,6]{2,1,0:T(2,128)} fusion(f32[2,6,3312]{1,0,2:T(2,128)S(1)} %copy.138, s32[21504]{0:T(1024)S(1)} %pad_clamp_fusion), kind=kCustom, calls=%fused_computation.1 | custom fusion | bytes 2073600 | tf_op jit(solution)/shard_map/jvp(jit(_take))/gather | solution.py:120
  81.6 31.1 %copy.139 = f32[144,144,2,6]{0,1,3,2:T(8,128)} copy(f32[144,144,2,6]{3,2,1,0:T(2,128)} %bitcast.176) | data formatting | bytes 1990656 | tf_op jit(solution)/shard_map/jvp(jit(_take))/gather | solution.py:120
  113.2 38.8 %gather_fusion.2 = f32[20736,12]{1,0:T(8,128)} fusion(f32[12,3312]{0,1:T(8,128)S(1)} %bitcast.170, s32[21504]{0:T(1024)S(1)} %pad_clamp_fusion), kind=kCustom, calls=%fused_computation.2 | custom fusion | bytes 2073600 | tf_op jit(solution)/shard_map/jvp(jit(_take))/gather | solution.py:120
  152.0 12.2 %copy.152 = f32[144,144,12]{0,1,2:T(8,128)} copy(f32[144,144,12]{2,1,0:T(8,128)} %bitcast.177) | data formatting | bytes 1990656 | tf_op jit(solution)/shard_map/jvp(jit(_take))/gather | solution.py:120
  164.9 5.6 collective-permute-start.1
  177.1 3.9 reshape.727
  181.1 2.7 copy.134
  183.8 2.6 fusion.95
  190.3 2.9 fusion.5
  194.2 3.5 convert_reduce_fusion
  197.8 3.0 copy.192
  200.8 2.7 fusion.23
  203.5 3.1 copy.141
  206.6 2.5 copy.142
  209.0 2.6 reshape.733
  217.1 3.4 collective-permute-start.2
  231.3 5.0 collective-permute-start.3
  285.1 3.0 fusion.86
  301.7 2.6 convolution_bitcast_fusion
  307.8 6.7 collective-permute-done.9
  320.6 3.1 copy.165
  323.7 3.0 copy.166
  326.7 3.4 fusion.3
  335.5 4.9 copy.171
  340.4 2.5 copy.172
  343.0 2.9 reshape.751
  351.6 274.9 %all-reduce.11.cloned.1.call-done = (f32[192,576]{1,0:T(8,128)}, f32[192,192]{1,0:T(8,128)}, f32[768,384]{1,0:T(8,128)}, f32[384,1152]{1,0:T(8,128)}, f32[384,384]{1,0:T(8,128)}) async-done(((f32[192,576]{1,0:T(8,128)}, f32[192,192]{1,0:T(8,128)}, f32[768,384]{1,0:T(8,128)}, f32[384,1152]{1,0:T(8,128)}, f32[384,384]{1,0:T(8,128)}), (f32[192,576]{1,0:T(8,128)}, f32[192,192]{1,0:T(8,128)}, ...) | async-done | bytes 4128784 | tf_op jit(solution)/shard_map/psum | solution.py:296
  629.4 4.3 collective-permute-done.4
  634.6 6.6 collective-permute-done.5
  642.4 6.8 collective-permute-done.11
  650.7 164.0 %all-reduce.13.cloned.1.call-done = (f32[192,576]{1,0:T(8,128)}, f32[192,192]{1,0:T(8,128)}, f32[768,384]{1,0:T(8,128)}, f32[384,1152]{1,0:T(8,128)}, f32[384,384]{1,0:T(8,128)}) async-done(((f32[192,576]{1,0:T(8,128)}, f32[192,192]{1,0:T(8,128)}, f32[768,384]{1,0:T(8,128)}, f32[384,1152]{1,0:T(8,128)}, f32[384,384]{1,0:T(8,128)}), (f32[192,576]{1,0:T(8,128)}, f32[192,192]{1,0:T(8,128)}, ...) | async-done | bytes 4128784 | tf_op jit(solution)/shard_map/psum | solution.py:295
  (350 shorter events, 144.9 us)
Async XLA Ops:
  7.2 11.0 %copy-start = (f32[8,12,3312]{2,0,1:T(8,128)S(1)}, f32[8,12,3312]{2,0,1:T(8,128)}, u32[]{:S(2)}) copy-start(f32[8,12,3312]{2,0,1:T(8,128)} %param.21) | copy-start | bytes 3815428
  7.2 8.2 copy-start.64
  7.2 4.6 copy-start.55
  7.2 8.2 copy-start.81
  7.2 619.3 %all-reduce.11.cloned.1.call-start = ((), (), s32[]{:S(2)}) async-start(), calls=%async_computation | async-start | bytes 8454144 | tf_op jit(solution)/shard_map/psum | solution.py:296
  9.6 10.1 %copy-start.18 = (f32[8,6,3312]{2,0,1:T(8,128)S(1)}, f32[8,6,3312]{2,0,1:T(8,128)}, u32[]{:S(2)}) copy-start(f32[8,6,3312]{2,0,1:T(8,128)} %param.20) | copy-start | bytes 1907716
  10.4 154.4 %collective-permute-start = (bf16[2,3,24,192]{3,2,1,0:T(8,128)(2,1)}, bf16[2,3,24,192]{3,2,1,0:T(8,128)(2,1)S(1)}, u32[]{:S(2)}, u32[]{:S(2)}) collective-permute-start(bf16[2,3,24,192]{3,2,1,0:T(8,128)(2,1)} %slice.192), channel_id=1, source_target_pairs={{1,0},{2,1},{3,2},{4,3},{5,4},{6,5},{7,6},{0,7},{9,8},{10,9},{11,1... | collective-permute-start | bytes 165896 | tf_op jit(solution)/shard_map/ppermute | solution.py:26
  13.2 157.3 %collective-permute-start.6 = (bf16[2,3,12,384]{3,2,1,0:T(8,128)(2,1)}, bf16[2,3,12,384]{3,2,1,0:T(8,128)(2,1)}, u32[]{:S(2)}, u32[]{:S(2)}) collective-permute-start(bf16[2,3,12,384]{3,2,1,0:T(8,128)(2,1)} %get-tuple-element.64), channel_id=1, source_target_pairs={{1,0},{2,1},{3,2},{4,3},{5,4},{6,5},{7,6},{0,7},{9,8},{10,9},{11,1... | collective-permute-start | bytes 165896 | tf_op jit(solution)/shard_map/ppermute | solution.py:26
  81.6 31.1 %copy-start.49 = (f32[1,12,3312]{2,0,1:T(1,128)S(1)}, f32[1,12,3312]{2,0,1:T(1,128)}, u32[]{:S(2)}) copy-start(f32[1,12,3312]{2,0,1:T(1,128)} %constant_dynamic-slice_fusion) | copy-start | bytes 476932
  152.0 12.2 %copy-start.69 = (f32[768]{0:T(1024)S(1)}, f32[768]{0:T(1024)}, u32[]{:S(2)}) copy-start(f32[768]{0:T(1024)} %param.23) | copy-start | bytes 9220
  152.0 12.8 %copy-start.29 = (bf16[2,9,24,192]{3,2,1,0:T(8,128)(2,1)S(1)}, bf16[2,9,24,192]{3,2,1,0:T(8,128)(2,1)}, u32[]{:S(2)}) copy-start(bf16[2,9,24,192]{3,2,1,0:T(8,128)(2,1)} %slice.191) | copy-start | bytes 497668
  152.0 18.4 %copy-start.59 = (bf16[2,3,12,384]{3,2,1,0:T(8,128)(2,1)S(1)}, bf16[2,3,12,384]{3,2,1,0:T(8,128)(2,1)}, u32[]{:S(2)}) copy-start(bf16[2,3,12,384]{3,2,1,0:T(8,128)(2,1)} %get-tuple-element.63) | copy-start | bytes 165892
  164.9 8.6 %collective-permute-start.1 = (bf16[2,12,6,192]{3,2,1,0:T(8,128)(2,1)S(1)}, bf16[2,12,6,192]{3,2,1,0:T(8,128)(2,1)S(1)}, u32[]{:S(2)}, u32[]{:S(2)}) collective-permute-start(bf16[2,12,6,192]{3,2,1,0:T(8,128)(2,1)S(1)} %pad_maximum_fusion.9), channel_id=1, source_target_pairs={{8,0},{16,8},{24,16},{32,24},{40,32},{48,40},{56,48},{64,56},{72,6... | collective-permute-start | bytes 165896 | tf_op jit(solution)/shard_map/ppermute | solution.py:26
  172.0 3.7 copy-start.46
  172.0 3.7 copy-start.75
  172.0 48.5 %collective-permute-start.7 = (bf16[2,6,6,384]{3,2,1,0:T(8,128)(2,1)}, bf16[2,6,6,384]{3,2,1,0:T(8,128)(2,1)}, u32[]{:S(2)}, u32[]{:S(2)}) collective-permute-start(bf16[2,6,6,384]{3,2,1,0:T(8,128)(2,1)} %get-tuple-element.62), channel_id=1, source_target_pairs={{8,0},{16,8},{24,16},{32,24},{40,32},{48,40},{56,48},{64,56},{72,6... | collective-permute-start | bytes 165896 | tf_op jit(solution)/shard_map/ppermute | solution.py:26
  217.1 13.3 %collective-permute-start.2 = (bf16[2,3,24,192]{3,2,1,0:T(8,128)(2,1)}, bf16[2,3,24,192]{3,2,1,0:T(8,128)(2,1)}, u32[]{:S(2)}, u32[]{:S(2)}) collective-permute-start(bf16[2,3,24,192]{3,2,1,0:T(8,128)(2,1)} %slice.199), channel_id=1, source_target_pairs={{1,0},{2,1},{3,2},{4,3},{5,4},{6,5},{7,6},{0,7},{9,8},{10,9},{11,1... | collective-permute-start | bytes 165896 | tf_op jit(solution)/shard_map/ppermute | solution.py:26
  231.3 7.2 collective-permute-start.3
  298.6 7.1 collective-permute-start.8
  301.7 3.8 copy-start.44
  304.3 11.1 %copy-start.58 = (bf16[192,192]{1,0:T(8,128)(2,1)S(1)}, bf16[192,192]{1,0:T(8,128)(2,1)}, u32[]{:S(2)}) copy-start(bf16[192,192]{1,0:T(8,128)(2,1)} %param.26) | copy-start | bytes 221188
  305.5 9.1 %copy-start.32 = (bf16[12,32,144]{2,1,0:T(8,128)(2,1)}, bf16[12,32,144]{2,1,0:T(8,128)(2,1)S(1)}, u32[]{:S(2)}) copy-start(bf16[12,32,144]{2,1,0:T(8,128)(2,1)S(1)} %convolution_convert_fusion.12) | copy-start | bytes 331780
  306.6 7.9 copy-start.30
  306.7 7.8 collective-permute-start.9
  351.5 463.2 %all-reduce.13.cloned.1.call-start = ((), (), s32[]{:S(2)}) async-start(), calls=%async_computation.1 | async-start | bytes 8454144 | tf_op jit(solution)/shard_map/psum | solution.py:295
  628.0 5.7 collective-permute-start.4
  633.7 7.5 collective-permute-start.5
  633.8 7.5 collective-permute-start.10
  641.4 7.8 collective-permute-start.11
  814.7 8.3 copy-start.17
  819.0 6.5 copy-start.14
  827.2 4.8 copy-start.1
  (64 other events, 106.5 us)
Sparse Core Ops, SparseCore 0:
  351.7 274.8 all-reduce.10
  629.6 185.0 all-reduce.12
